TPU v7x, 32 devices: a whole 2x2x4 slice. The times are simulated.
32 devices in a mesh: hst: 4 (over y, x), chip: 8 (over z, core).
Axes of the slice: x: 2, y: 2, z: 4, core: 2. Of those that a mesh axis runs over, the one named last changes fastest.
Arguments:
- resident_row_blocks: bfloat16 [1536, 128, 128], P(('hst', 'chip')), may hold values from -3 to 3
- orphan_blocks: bfloat16 [1024, 128, 128], P(('hst', 'chip')), may hold values from -3 to 3
- home_offsets: int32 [1536, 32, 8], P(('hst', 'chip')), may hold values from 0 to 127
- home_lengths: int32 [1536, 32], P(('hst', 'chip')), may hold values from 1 to 8
- home_samples: int32 [1536, 32], P(('hst', 'chip')), may hold values from 0 to 511
- orphan_offsets: int32 [1024, 32, 8], P(('hst', 'chip')), may hold values from 0 to 127
- orphan_lengths: int32 [1024, 32], P(('hst', 'chip')), may hold values from 1 to 8
- orphan_samples: int32 [1024, 32], P(('hst', 'chip')), may hold values from 0 to 511
- orphan_owner: int32 [1024, 1], P(('hst', 'chip')), may hold values from 0 to 7; in each aligned block of 32 rows (0 to 31, 32 to 63, ...) at most 8 rows name the same one
- dense_inputs: bfloat16 [16384, 13], P(('hst', 'chip')), may hold values from -6 to 6
- labels: int32 [16384], P(('hst', 'chip')), may hold values 0 or 1
- bottom_first: bfloat16 [13, 512], replicated, may hold values from -1.75 to 1.75
- bias_first: float32 [512], replicated, may hold values from -1.5 to 1.5
- bottom_second: bfloat16 [512, 256], replicated, may hold values from -0.375 to 0.375
- bias_second: float32 [256], replicated, may hold values from -1.5 to 1.5
- bottom_third: bfloat16 [256, 128], replicated, may hold values from -0.5 to 0.5
- bias_third: float32 [128], replicated, may hold values from -1.5 to 1.5
- top_hidden: bfloat16 [479, 1024], replicated, may hold values from -0.125 to 0.125
- bias_hidden: float32 [1024], replicated, may hold values from -1.5 to 1.5
- top_logit: bfloat16 [1024, 1], replicated, may hold values from -0.25 to 0.25
- bias_logit: float32 [1], replicated, may hold values from -3 to 3
Outputs:
- rehomed: bfloat16 [2048, 128, 128], P(('hst', 'chip'))
- logits: float32 [16384], P(('hst', 'chip'))
- loss: float32 [], replicated
Inputs may be any that keep to these rules, and one draw needn't show every extreme that they name: `orphan_owner`: among the 32 orphans of one device at most 8 have the same new owner; some holder and owner reach 8.
All inputs are finite; a program needn't handle non-finite values. No bound on the sum of `labels` on one device may be relied on, other than what follows from the above.
Results may differ from a plain program's by a relative error of at most 0.0079.
Values may be sent and summed in bfloat16 or wider, within the bound.
A program may use at most 128 MiB of HBM per device.

v0:
```python
import functools

import jax
import jax.numpy as jnp
from jax import lax
from jax.experimental import pallas as pl
from jax.experimental.pallas import tpu as pltpu
from jax.sharding import PartitionSpec as P

F = 26
CORES = 2
CHUNKS = 3
SLAB = 32
VM, HBM, SMEM = pltpu.VMEM, pltpu.HBM, pltpu.SMEM
F32, BF16, I32 = jnp.float32, jnp.bfloat16, jnp.int32
MESH = pl.DeviceIdType.MESH


def cost(flops, bytes_accessed):
    return pl.CostEstimate(flops=flops, bytes_accessed=bytes_accessed, transcendentals=0)


def nt(a, b):
    return lax.dot_general(a, b, (((1,), (1,)), ((), ())), preferred_element_type=F32)


def mm(a, b):
    return jnp.dot(a, b, preferred_element_type=F32)


def turn(j, half):
    if j >= half - CORES:
        return 0, half - 1 - j
    return 1 + j // CORES, j % CORES


def walk(chip, half, side, a, b):
    per = half // CORES
    base, local = lax.div(chip, half), lax.rem(chip, half)
    base = lax.rem(base + side, 2) * half
    return base + lax.rem(lax.div(local, CORES) + a, per) * CORES + lax.rem(local + b, CORES)


NAMES = (
    "owner", "orph", "home", "hoff", "ooff", "hlen", "olen", "hsamp", "osamp",
    "dense", "w1", "b1", "w2", "b2", "w3", "b3", "wt", "bh", "wl", "label",
)


def step_kernel(hosts, chips, slots, cap, depth, *refs):
    half = chips // 2
    devices = hosts * chips
    bl_ref = refs[0]
    hbm = dict(zip(NAMES, refs[1:1 + len(NAMES)]))
    refs = refs[1 + len(NAMES):]
    rehomed, logit_ref, loss_ref, over_ref = refs[:4]
    v = dict(zip(NAMES, refs[4:4 + len(NAMES)]))
    (packed, relay, held, fwd, meta_send, meta, stage, counts, rows, out_rows, arrived, pieces, slab, gram, wpad, wexp,
     order, loss_send, losses,
     in_sems, meta_s, meta_r, row_s, row_r, loss_s, loss_r, list_s, list_r, near_s, near_r, fwd_s, fwd_r,
     own_sems) = refs[4 + len(NAMES):]

    homes, height = v["home"].shape[0], v["home"].shape[1]
    orphs = v["orph"].shape[0]
    count = homes + orphs
    total = devices * count
    width = v["home"].shape[2]
    batch = logit_ref.shape[1]
    part = cap // CHUNKS

    host, chip = lax.axis_index("hst"), lax.axis_index("chip")
    me = host * chips + chip
    mirror = lax.rem(chip + half, chips)

    def peer(e):
        side, e = lax.div(e, hosts * half), lax.rem(e, hosts * half)
        dh, e = lax.div(e, half), lax.rem(e, half)
        return lax.rem(host + dh, hosts), walk(chip, half, side, lax.div(e, CORES), lax.rem(e, CORES))

    bar = pltpu.get_barrier_semaphore()

    def hello(e, carry):
        pl.semaphore_signal(bar, 1, device_id=peer(e), device_id_type=MESH)
        return carry

    lax.fori_loop(1, devices, hello, 0)

    loads = {n: pltpu.make_async_copy(hbm[n], v[n], in_sems.at[k]) for k, n in enumerate(NAMES)}
    for n in NAMES:
        loads[n].start()

    def everyone(src, dst, send, recv, indexed):
        def copy(e):
            h, c = peer(e)
            return pltpu.make_async_remote_copy(
                src_ref=src.at[h * chips + c] if indexed else src.at[0],
                dst_ref=dst.at[me], send_sem=send.at[e], recv_sem=recv.at[e],
                device_id=(h, c), device_id_type=MESH)

        def start():
            def go(i, carry):
                copy(devices - i).start()
                return carry
            lax.fori_loop(1, devices, go, 0)

        def wait(kind):
            def go(i, carry):
                c = copy(devices - i)
                c.wait_recv() if kind == "recv" else c.wait_send()
                return carry
            lax.fori_loop(1, devices, go, 0)

        return start, wait

    meta_go, meta_wait = everyone(meta_send, meta, meta_s, meta_r, True)
    rows_go, rows_wait = everyone(out_rows, arrived, row_s, row_r, True)
    loss_go, loss_wait = everyone(loss_send, losses, loss_s, loss_r, False)

    lists = [
        pltpu.make_async_remote_copy(
            src_ref=packed.at[pl.ds(half * slots + k * part, part)],
            dst_ref=relay.at[pl.ds(k * part, part)],
            send_sem=list_s.at[k], recv_sem=list_r.at[k], device_id=(host, mirror), device_id_type=MESH)
        for k in range(CHUNKS)
    ]

    def group(src, holder, j, send, recv):
        return pltpu.make_async_remote_copy(
            src_ref=src.at[pl.ds(j * slots, slots)],
            dst_ref=rehomed.at[pl.ds(holder * slots, slots)],
            send_sem=send.at[j], recv_sem=recv.at[j],
            device_id=(host, walk(chip, half, 0, *turn(j, half))), device_id_type=MESH)

    near = [group(packed, chip, j, near_s, near_r) for j in range(half - 1)]
    onward = [group(fwd, mirror, j, fwd_s, fwd_r) for j in range(half - 1)]
    own = [
        pltpu.make_async_copy(ref.at[pl.ds((half - 1) * slots, slots)],
                              rehomed.at[pl.ds(holder * slots, slots)], own_sems.at[k])
        for k, (ref, holder) in enumerate(((packed, chip), (fwd, mirror)))
    ]

    loads["owner"].wait()
    to = v["owner"][...]
    key = jnp.zeros_like(to)
    for side in range(2):
        for j in range(half):
            key = jnp.where(to == walk(chip, half, side, *turn(j, half)), side * half + j, key)
    tag = lax.broadcasted_iota(I32, to.shape, 1)
    square = (orphs, orphs)
    code = jnp.broadcast_to((key * orphs + tag).astype(F32), square)
    kind = jnp.broadcast_to(key.astype(F32), square)
    rank = jnp.sum((code.T < code).astype(F32), axis=0, keepdims=True).astype(I32)
    prefix = jnp.sum((kind.T < kind).astype(F32), axis=0, keepdims=True).astype(I32)
    inside = jnp.sum((kind.T < half).astype(F32), axis=0, keepdims=True).astype(I32)
    place = jnp.where(key < half, key * slots + rank - prefix, half * slots + rank - inside)
    sizes = [jnp.sum((key == half + j).astype(I32)) for j in range(half)]
    sizes.append(jnp.sum((key >= half).astype(I32)))
    loads["orph"].wait()

    def pack(first_at, number):
        for t in range(first_at, first_at + number):
            found = jnp.sum(jnp.where(place == t, tag + 1, 0))
            block = v["orph"][jnp.maximum(found - 1, 0)]
            packed[t] = jnp.where(found > 0, block, jnp.zeros_like(block))

    pack(half * slots, part)
    pl.semaphore_wait(bar, devices - 1)
    lists[0].start()
    pack(0, half * slots)
    near[half - CORES].start()
    near[0].start()
    own[0].start()
    pack(half * slots + part, cap - part)

    stage[...] = jnp.zeros_like(stage)
    loads["osamp"].wait()
    stage[0:orphs, 0:devices] = v["osamp"][...].astype(F32)
    turned = stage[...].T[0:devices].astype(I32)
    lane = lax.broadcasted_iota(I32, (devices, 128), 1)
    rest = pltpu.roll(turned, homes, 1)
    loads["hsamp"].wait()
    stage[0:devices, 0:homes] = v["hsamp"][...].astype(F32)
    line = jnp.where(lane < homes, stage[0:devices].astype(I32), rest)
    for j in range(half + 1):
        line = jnp.where(lane == count + j, sizes[j], line)
    for p in range(devices):
        meta_send[p] = line[p:p + 1]
    meta[me] = meta_send[me]

    meta_go()

    row = lax.broadcasted_iota(I32, (height, 128), 0)
    bag = hbm["hoff"].shape[1]

    def hits(off):
        found = jnp.zeros((height, 128), F32)
        for k in range(bag):
            found = found + (row == off[k:k + 1]).astype(F32)
        return found.T

    for n in ("hoff", "hlen"):
        loads[n].wait()
    slot = lax.broadcasted_iota(I32, (bag, homes), 0)
    blank = jnp.full((bag, 64 - homes), height, I32)

    def pair(g, carry):
        off = []
        for k in range(2):
            p = g * 2 + k
            off += [jnp.where(slot < v["hlen"][pl.ds(p, 1), :], v["hoff"][p], height), blank]
        found = hits(jnp.concatenate(off, axis=1))
        for k in range(2):
            counts[pl.ds(pl.multiple_of((g * 2 + k) * homes, 8), homes), :] = found[k * 64:k * 64 + homes]
        return carry

    lax.fori_loop(0, devices // 2, pair, 0)
    loads["home"].wait()

    def home_piece(b, carry):
        lhs = counts[pl.ds(b, devices, stride=homes), :].astype(BF16)
        rows[pl.ds(b, devices, stride=count), :] = mm(lhs, v["home"][b])
        return carry

    lax.fori_loop(0, homes, home_piece, 0, unroll=4)
    for n in ("ooff", "olen"):
        loads[n].wait()
    per = 128 // devices
    spot = lax.broadcasted_iota(I32, (bag, devices), 0)

    def orph_group(g, carry):
        off = []
        for k in range(per):
            b = g * per + k
            off.append(jnp.where(spot < v["olen"][pl.ds(b, 1), :], v["ooff"][b], height))
        found = hits(jnp.concatenate(off, axis=1) if per > 1 else off[0]).astype(BF16)
        for k in range(per):
            b = g * per + k
            rows[pl.ds(homes + b, devices, stride=count), :] = mm(found[k * devices:(k + 1) * devices], v["orph"][b])
        return carry

    lax.fori_loop(0, orphs // per, orph_group, 0)
    out_rows[...] = rows[...].reshape(out_rows.shape).astype(BF16)
    rows_go()
    arrived[me] = out_rows[me]
    for j in range(1, half - CORES):
        near[j].start()
    for k in range(1, CHUNKS):
        lists[k].start()
    for j in range(half - CORES + 1, half - 1):
        near[j].start()

    for n in NAMES[9:]:
        loads[n].wait()
    inter = v["wt"].shape[0]
    whole = inter // 16 * 16
    wpad[whole:, :] = jnp.zeros((wpad.shape[0] - whole, wpad.shape[1]), BF16)
    wpad[0:inter, :] = v["wt"][...]
    cell = lax.broadcasted_iota(I32, (SLAB * SLAB, wpad.shape[0]), 0)
    i, j = cell // SLAB, cell % SLAB
    column = lax.broadcasted_iota(I32, cell.shape, 1)
    pick = (column == 128 + i * (i - 1) // 2 + j) & (j < i) & (i <= F)
    wexp[...] = mm(jnp.where(pick, 1.0, 0.0).astype(BF16), wpad[...]).astype(BF16)

    first = lax.dot_general(v["dense"][...], v["w1"][...], (((0,), (0,)), ((), ())), preferred_element_type=F32)
    first = jnp.maximum(first + v["b1"][...], 0.0).astype(BF16)
    second = jnp.maximum(mm(first, v["w2"][...]) + v["b2"][...], 0.0).astype(BF16)
    slab[0] = jnp.maximum(mm(second, v["w3"][...]) + v["b3"][...], 0.0)
    slab[F + 1:] = jnp.zeros((SLAB - F - 1,) + slab.shape[1:], F32)

    meta_wait("recv")
    bits = meta[host * chips + mirror]
    here = lax.broadcasted_iota(I32, bits.shape, 1)
    tops = [jnp.sum(jnp.where(here == count + k, bits, 0)) for k in range(half)]

    def forward(j):
        first_at = sum(tops[:j]) if j else 0

        def go(s, carry):
            at = jnp.minimum(first_at + s, cap - 1)
            fwd[j * slots + s] = jnp.where(s < tops[j], held[at], jnp.zeros(held.shape[1:], BF16))
            return carry

        lax.fori_loop(0, slots, go, 0)
        if j < half - 1:
            onward[j].start()
        else:
            own[1].start()

    def last_chunk(j):
        return (min(cap, (j + 1) * slots) - 1) // part

    at_lane = lax.broadcasted_iota(I32, (1, 128), 1)
    for d in range(depth):
        values = jnp.full((1, 128), -1, I32)
        n = d * F
        while n < min((d + 1) * F, total):
            if n < devices * homes:
                p, s = n // homes, n % homes
                size = homes - s
            else:
                p, s = (n - devices * homes) // orphs, (n - devices * homes) % orphs
                size = orphs - s
                s = homes + s
            to = n - d * F
            size = min(size, F - to)
            moved = pltpu.roll(meta[p], (to - s) % 128, 1) if to != s else meta[p]
            values = jnp.where((at_lane >= to) & (at_lane < to + size), moved, values)
            n += size
        order[d:d + 1, :] = values.astype(F32)
    where = order[...].T[0:SLAB].astype(I32)

    def unpack(k):
        lists[k].wait_recv()
        held[k * part:(k + 1) * part] = relay[k * part:(k + 1) * part]
        for j in range(half):
            if last_chunk(j) == k:
                forward(j)

    unpack(0)

    pieces[total:, :] = jnp.zeros((pieces.shape[0] - total, pieces.shape[1]), F32)
    rows_wait("recv")

    def settle(p, carry):
        pieces[pl.ds(pl.multiple_of(p * homes, 8), homes), :] = arrived[p, 0:homes].astype(F32)
        pieces[pl.ds(pl.multiple_of(devices * homes + p * orphs, 8), orphs), :] = (
            arrived[p, homes:count].astype(F32))
        return carry

    lax.fori_loop(0, devices, settle, 0, unroll=2)

    sample = lax.broadcasted_iota(I32, (batch, depth), 0)
    for f in range(F):
        mine = pieces[pl.ds(f, depth, stride=F), :].astype(BF16)
        hot = jnp.where(sample == where[f:f + 1, :], 1.0, 0.0).astype(BF16)
        slab[f + 1] = mm(hot, mine)

    edge = SLAB * 8
    same = (lax.broadcasted_iota(I32, (edge, edge), 0) % 8) == (
        lax.broadcasted_iota(I32, (edge, edge), 1) % 8)

    def products(g, carry):
        halves = []
        for k in range(2):
            at = pl.ds(pl.multiple_of(g * 16 + k * 8, 8), 8)
            x = slab[:, at, :].reshape(edge, slab.shape[2]).astype(BF16)
            halves.append(jnp.where(same, nt(x, x), 0.0).reshape(SLAB, 8, edge))
        both = jnp.concatenate(halves, axis=1).astype(BF16)
        gram[:, pl.ds(pl.multiple_of(g * 16, 16), 16), :] = both
        return carry

    lax.fori_loop(0, batch // 16, products, 0, unroll=2)

    lane_j = lax.broadcasted_iota(I32, (edge, edge), 0) // 8
    out_lane = lax.broadcasted_iota(I32, (edge, edge), 1)
    features = []
    for h in range(SLAB // 8):
        acc = None
        for k in range(8):
            i_ = h * 8 + k
            if i_ < 1 or i_ > F:
                continue
            live = 128 if i_ <= 16 else edge
            fold_ = jnp.where(lane_j + k * SLAB == out_lane, 1.0, 0.0).astype(BF16)
            term = mm(gram[i_, :, 0:live], fold_[0:live])
            acc = term if acc is None else acc + term
        features.append(acc.astype(BF16))
    bottom = slab[0].astype(BF16)

    tally = jnp.zeros((batch, 128), F32)
    step = 256
    scale = v["wl"][...].astype(F32)
    for n in range(0, wpad.shape[1], step):
        pre = mm(bottom, wpad[0:128, n:n + step])
        for h in range(SLAB // 8):
            pre = pre + mm(features[h], wexp[h * 256:(h + 1) * 256, n:n + step])
        hidden = jnp.maximum(pre + v["bh"][:, n:n + step], 0.0).astype(BF16).astype(F32)
        scaled = hidden * scale[:, n:n + step]
        tally = tally + scaled[:, 0:128] + scaled[:, 128:256]
    logits = jnp.sum(tally.T, axis=0, keepdims=True) + bl_ref[0]
    logit_ref[...] = logits
    soft = jnp.maximum(logits, 0.0) + jnp.log1p(jnp.exp(-jnp.abs(logits)))
    loss = jnp.sum(soft - v["label"][...].astype(F32) * logits, axis=1, keepdims=True)
    loss_send[0] = jnp.broadcast_to(loss, (1, 128))
    losses[me] = loss_send[0]
    loss_go()

    for k in range(1, CHUNKS):
        unpack(k)

    crossing = jnp.where(at_lane == count + half, jnp.max(meta[...].astype(F32), axis=0), 0.0)
    over_ref[0] = (jnp.max(crossing) > cap).astype(I32)
    loss_wait("recv")
    loss_ref[0] = jnp.sum(jnp.where(at_lane == 0, jnp.sum(losses[...], axis=0), 0.0))

    meta_wait("send")
    rows_wait("send")
    loss_wait("send")
    for c in lists:
        c.wait_send()
    for c in near + onward:
        c.wait()
    for c in own:
        c.wait()


def step(hosts, chips, slots, bl, arrays):
    devices = hosts * chips
    half = chips // 2
    home, orph = arrays["home"], arrays["orph"]
    homes, height, width = home.shape
    orphs = orph.shape[0]
    count = homes + orphs
    batch = arrays["dense"].shape[1]
    top = arrays["wt"].shape[1]
    cap = -(-3 * orphs // (4 * CHUNKS)) * CHUNKS
    total = devices * count
    depth = -(-total // (F * 128)) * 128
    dma = pltpu.SemaphoreType.DMA
    scratch = [VM(arrays[n].shape, arrays[n].dtype) for n in NAMES] + [
        VM((half * slots + cap, height, width), BF16),
        VM((cap, height, width), BF16),
        VM((cap, height, width), BF16),
        VM((half * slots, height, width), BF16),
        VM((devices, 1, 128), I32),
        VM((devices, 1, 128), I32),
        VM((128, 128), F32),
        VM((devices * homes, height), F32),
        VM((devices * count, width), F32),
        VM((devices, count, width), BF16),
        VM((devices, count, width), BF16),
        VM((F * depth, width), F32),
        VM((SLAB, batch, width), F32),
        VM((SLAB, batch, SLAB * 8), BF16),
        VM((512, top), BF16),
        VM((SLAB * SLAB, top), BF16),
        VM((depth, 128), F32),
        VM((1, 1, 128), F32),
        VM((devices, 1, 128), F32),
        dma((len(NAMES),)),
        dma((devices,)), dma((devices,)), dma((devices,)), dma((devices,)), dma((devices,)), dma((devices,)),
        dma((CHUNKS,)), dma((CHUNKS,)),
        dma((half,)), dma((half,)), dma((half,)), dma((half,)),
        dma((2,)),
    ]
    smem, hbm, vmem = (pl.BlockSpec(memory_space=m) for m in (SMEM, HBM, VM))
    return pl.pallas_call(
        functools.partial(step_kernel, hosts, chips, slots, cap, depth),
        out_shape=(
            jax.ShapeDtypeStruct((chips * slots, height, width), BF16),
            jax.ShapeDtypeStruct((1, batch), F32),
            jax.ShapeDtypeStruct((1,), F32),
            jax.ShapeDtypeStruct((1,), I32),
        ),
        in_specs=[smem] + [hbm] * len(NAMES),
        out_specs=(hbm, vmem, smem, smem),
        scratch_shapes=scratch,
        cost_estimate=cost(8_000_000_000, 8_000_000),
        compiler_params=pltpu.CompilerParams(
            collective_id=0, has_side_effects=True, vmem_limit_bytes=56 * 2**20),
        name="step",
    )(bl, *[arrays[n] for n in NAMES])


def padded(owners, blocks, chips, slots):
    number = blocks.shape[0]
    index = jnp.arange(number, dtype=I32)
    earlier = index[None, :] < index[:, None]
    rank = jnp.sum(((owners[:, None] == owners[None, :]) & earlier).astype(I32), axis=1)
    match = (owners * slots + rank)[None, :] == jnp.arange(chips * slots, dtype=I32)[:, None]
    source = jnp.sum(match.astype(I32) * index[None, :], axis=1)
    filled = jnp.any(match, axis=1)
    groups = jnp.where(filled[:, None, None], blocks[source], jnp.zeros((), BF16))
    return lax.all_to_all(groups, "chip", split_axis=0, concat_axis=0, tiled=True)


def per_device(
    resident_row_blocks,
    orphan_blocks,
    home_offsets,
    home_lengths,
    home_samples,
    orphan_offsets,
    orphan_lengths,
    orphan_samples,
    orphan_owner,
    dense_inputs,
    labels,
    bottom_first,
    bias_first,
    bottom_second,
    bias_second,
    bottom_third,
    bias_third,
    top_hidden,
    bias_hidden,
    top_logit,
    bias_logit,
):
    hosts, chips = lax.axis_size("hst"), lax.axis_size("chip")
    orphs = orphan_blocks.shape[0]
    slots = (2 * orphs + chips - 1) // chips
    owners = orphan_owner[:, 0]
    arrays = dict(
        owner=orphan_owner.T, home=resident_row_blocks, orph=orphan_blocks,
        hoff=home_offsets.transpose(1, 2, 0), ooff=orphan_offsets.transpose(0, 2, 1),
        hlen=home_lengths.T, olen=orphan_lengths, hsamp=home_samples.T, osamp=orphan_samples,
        dense=dense_inputs.T, w1=bottom_first, b1=bias_first[None], w2=bottom_second, b2=bias_second[None],
        w3=bottom_third, b3=bias_third[None], wt=top_hidden, bh=bias_hidden[None], wl=top_logit.T,
        label=labels[None],
    )
    rehomed, logits, loss, over = step(hosts, chips, slots, bias_logit, arrays)
    rehomed = lax.cond(
        over[0] > 0,
        lambda r, o, b: padded(o, b, chips, slots),
        lambda r, o, b: r,
        rehomed, owners, orphan_blocks,
    )
    return rehomed, logits[0], loss[0]


def solution(mesh):
    both = ("hst", "chip")
    three, two = P(both, None, None), P(both, None)
    return jax.shard_map(
        per_device,
        mesh=mesh,
        in_specs=(three, three, three, two, two, three, two, two, two, two, P(both)) + (P(),) * 10,
        out_specs=(three, P(both), P()),
        check_vma=False,
    )
```

profile of v0, /device:TPU:1, one launch (start us, length us, event | category | flops | bytes accessed | tf_op | source)
XLA Modules:
  0.0 67.9 jit_solution(569516224917320460)
XLA Ops:
  1.3 0.0 copy-start
  1.3 0.0 copy-start.2
  1.3 62.4 %step.1 = (bf16[64,128,128]{2,1,0:T(8,128)(2,1)S(1)}, f32[1,512]{1,0:T(1,128)}, f32[1]{0:T(128)}, s32[1]{0:T(128)}) custom-call(f32[1]{0:T(128)S(6)} %copy.29.refs_0_, s32[1,32]{1,0:T(1,128)} %bitcast.34, bf16[32,128,128]{2,1,0:T(8,128)(2,1)} %refs_2_.1, bf16[48,128,128]{2,1,0:T(8,128)(2,1)} %refs_3_.1, s32[32,8,48]{2,1,0:T(8,128)} %bitcast.23, ...), custom_call_target="tpu_custom_call" | custom-call | flops 8000000000 | bytes 8000000 | tf_op jit(solution)/shard_map/step/pallas_call | solution.py:447
  64.3 0.0 copy-done
  64.3 0.0 copy-done.2
  64.3 0.0 copy-start.1
  64.4 1.3 %copy.30 = bf16[64,128,128]{2,1,0:T(8,128)(2,1)} copy(bf16[64,128,128]{2,1,0:T(8,128)(2,1)S(1)} %get-tuple-element.31) | data formatting | bytes 4194304
  65.7 0.0 copy-done.1
  65.7 0.6 copy.31
  (1 shorter events, 0.0 us)
Async XLA Ops:
  1.3 63.0 %copy-start = (bf16[32,128,128]{2,1,0:T(8,128)(2,1)S(1)}, bf16[32,128,128]{2,1,0:T(8,128)(2,1)}, u32[]{:S(2)}) copy-start(bf16[32,128,128]{2,1,0:T(8,128)(2,1)} %refs_2_.1) | copy-start | bytes 3145732
  1.3 63.0 %copy-start.2 = (s32[32,1]{0,1:T(1,128)S(1)}, s32[32,1]{0,1:T(1,128)}, u32[]{:S(2)}) copy-start(s32[32,1]{0,1:T(1,128)} %param.31) | copy-start | bytes 388
  64.3 1.3 %copy-start.1 = (f32[1,512]{1,0:T(1,128)S(1)}, f32[1,512]{1,0:T(1,128)}, u32[]{:S(2)}) copy-start(f32[1,512]{1,0:T(1,128)} %get-tuple-element.22) | copy-start | bytes 6148
where the time goes:
time: 68.1 us; the launch traced here: 67.9 us
  Pallas kernels  62.4 us (92%)
  between operations  3.67 us (5%)
  local copies, waits for them, and re-layouts  1.91 us (3%)
    pallas_call x1, Pallas kernels, step(): pl.pallas_call(functools.partial(step_kernel, hosts, chips, slots, cap, d...  62.4 us
    unnamed x8, local copies, waits for them, and re-layouts  1.91 us

commit v1 on v0

--- a/solution.py
+++ b/solution.py
@@ -9,7 +9,7 @@
 
 F = 26
 CORES = 2
-CHUNKS = 3
+PAIR = 2
 SLAB = 32
 VM, HBM, SMEM = pltpu.VMEM, pltpu.HBM, pltpu.SMEM
 F32, BF16, I32 = jnp.float32, jnp.bfloat16, jnp.int32
@@ -39,6 +39,18 @@
     base, local = lax.div(chip, half), lax.rem(chip, half)
     base = lax.rem(base + side, 2) * half
     return base + lax.rem(lax.div(local, CORES) + a, per) * CORES + lax.rem(local + b, CORES)
+
+
+def passes(half, slots, ends):
+    found = []
+    for j in range(half):
+        low = 0
+        for k, end in enumerate(ends):
+            high = slots if k == len(ends) - 1 else min(slots, end - j * slots)
+            if high > low:
+                found.append((k, j, low, high))
+                low = high
+    return sorted(found)
 
 
 NAMES = (
@@ -58,7 +70,7 @@
     (packed, relay, held, fwd, meta_send, meta, stage, counts, rows, out_rows, arrived, pieces, slab, gram, wpad, wexp,
      order, loss_send, losses,
      in_sems, meta_s, meta_r, row_s, row_r, loss_s, loss_r, list_s, list_r, near_s, near_r, fwd_s, fwd_r,
-     own_sems) = refs[4 + len(NAMES):]
+     own_sem) = refs[4 + len(NAMES):]
 
     homes, height = v["home"].shape[0], v["home"].shape[1]
     orphs = v["orph"].shape[0]
@@ -66,11 +78,22 @@
     total = devices * count
     width = v["home"].shape[2]
     batch = logit_ref.shape[1]
-    part = cap // CHUNKS
+    quarter = orphs // 8
+    ends = [2 * quarter, 3 * quarter, 4 * quarter, cap]
+    starts = [0] + ends[:-1]
+    steps = len(ends)
 
     host, chip = lax.axis_index("hst"), lax.axis_index("chip")
     me = host * chips + chip
-    mirror = lax.rem(chip + half, chips)
+    my_half = lax.div(chip, half)
+    local, core = lax.div(lax.rem(chip, half), CORES), lax.rem(chip, CORES)
+    low_chip = lax.div(local, PAIR) * PAIR
+    gate = lax.rem(local, PAIR) == 1 - my_half
+    half_chips = half // CORES
+    across = (1 - my_half) * half
+    target = across + (low_chip + my_half) * CORES + core
+    holders = [across + (low_chip + i) * CORES + core for i in range(PAIR)]
+    turn_in = lax.rem(local, PAIR)
 
     def peer(e):
         side, e = lax.div(e, hosts * half), lax.rem(e, hosts * half)
@@ -118,33 +141,48 @@
 
     lists = [
         pltpu.make_async_remote_copy(
-            src_ref=packed.at[pl.ds(half * slots + k * part, part)],
-            dst_ref=relay.at[pl.ds(k * part, part)],
-            send_sem=list_s.at[k], recv_sem=list_r.at[k], device_id=(host, mirror), device_id_type=MESH)
-        for k in range(CHUNKS)
+            src_ref=packed.at[pl.ds(half * slots + starts[k], ends[k] - starts[k])],
+            dst_ref=relay.at[turn_in, pl.ds(starts[k], ends[k] - starts[k])],
+            send_sem=list_s.at[k], recv_sem=list_r.at[turn_in, k],
+            device_id=(host, target), device_id_type=MESH)
+        for k in range(steps)
     ]
 
-    def group(src, holder, j, send, recv):
+    def listed(i, k):
+        size = ends[k] - starts[k]
         return pltpu.make_async_remote_copy(
-            src_ref=src.at[pl.ds(j * slots, slots)],
-            dst_ref=rehomed.at[pl.ds(holder * slots, slots)],
-            send_sem=send.at[j], recv_sem=recv.at[j],
+            src_ref=packed.at[pl.ds(half * slots + starts[k], size)],
+            dst_ref=relay.at[i, pl.ds(starts[k], size)],
+            send_sem=list_s.at[k], recv_sem=list_r.at[i, k],
+            device_id=(host, target), device_id_type=MESH)
+
+    def group(src, holder, j, low, high, send, recv):
+        return pltpu.make_async_remote_copy(
+            src_ref=src.at[pl.ds(j * slots + low, high - low)],
+            dst_ref=rehomed.at[pl.ds(holder * slots + low, high - low)],
+            send_sem=send, recv_sem=recv,
             device_id=(host, walk(chip, half, 0, *turn(j, half))), device_id_type=MESH)
 
-    near = [group(packed, chip, j, near_s, near_r) for j in range(half - 1)]
-    onward = [group(fwd, mirror, j, fwd_s, fwd_r) for j in range(half - 1)]
-    own = [
-        pltpu.make_async_copy(ref.at[pl.ds((half - 1) * slots, slots)],
-                              rehomed.at[pl.ds(holder * slots, slots)], own_sems.at[k])
-        for k, (ref, holder) in enumerate(((packed, chip), (fwd, mirror)))
-    ]
+    near = [group(packed, chip, j, 0, slots, near_s.at[j], near_r.at[j]) for j in range(half - 1)]
+    onward = {}
+    for n, (k, j, low, high) in enumerate(passes(half, slots, ends)):
+        for i in range(PAIR):
+            if j < half - 1:
+                onward[i, k, j] = group(fwd.at[i], holders[i], j, low, high, fwd_s.at[i, n], fwd_r.at[i, n])
+            else:
+                onward[i, k, j] = pltpu.make_async_copy(
+                    fwd.at[i, pl.ds(j * slots + low, high - low)],
+                    rehomed.at[pl.ds(holders[i] * slots + low, high - low)], fwd_s.at[i, n])
+    own = pltpu.make_async_copy(packed.at[pl.ds((half - 1) * slots, slots)],
+                                rehomed.at[pl.ds(chip * slots, slots)], own_sem)
 
     loads["owner"].wait()
     to = v["owner"][...]
     key = jnp.zeros_like(to)
     for side in range(2):
         for j in range(half):
-            key = jnp.where(to == walk(chip, half, side, *turn(j, half)), side * half + j, key)
+            owner = walk(target if side else chip, half, 0, *turn(j, half))
+            key = jnp.where(to == owner, side * half + j, key)
     tag = lax.broadcasted_iota(I32, to.shape, 1)
     square = (orphs, orphs)
     code = jnp.broadcast_to((key * orphs + tag).astype(F32), square)
@@ -163,14 +201,17 @@
             block = v["orph"][jnp.maximum(found - 1, 0)]
             packed[t] = jnp.where(found > 0, block, jnp.zeros_like(block))
 
-    pack(half * slots, part)
+    pack(half * slots, ends[0])
     pl.semaphore_wait(bar, devices - 1)
     lists[0].start()
+    pack(half * slots + starts[1], ends[1] - starts[1])
+    lists[1].start()
     pack(0, half * slots)
-    near[half - CORES].start()
     near[0].start()
-    own[0].start()
-    pack(half * slots + part, cap - part)
+    for j in range(half - CORES, half - 1):
+        near[j].start()
+    own.start()
+    pack(half * slots + starts[2], cap - starts[2])
 
     stage[...] = jnp.zeros_like(stage)
     loads["osamp"].wait()
@@ -242,11 +283,9 @@
     out_rows[...] = rows[...].reshape(out_rows.shape).astype(BF16)
     rows_go()
     arrived[me] = out_rows[me]
+    for k in range(2, steps):
+        lists[k].start()
     for j in range(1, half - CORES):
-        near[j].start()
-    for k in range(1, CHUNKS):
-        lists[k].start()
-    for j in range(half - CORES + 1, half - 1):
         near[j].start()
 
     for n in NAMES[9:]:
@@ -268,26 +307,27 @@
     slab[F + 1:] = jnp.zeros((SLAB - F - 1,) + slab.shape[1:], F32)
 
     meta_wait("recv")
-    bits = meta[host * chips + mirror]
-    here = lax.broadcasted_iota(I32, bits.shape, 1)
-    tops = [jnp.sum(jnp.where(here == count + k, bits, 0)) for k in range(half)]
-
-    def forward(j):
-        first_at = sum(tops[:j]) if j else 0
-
-        def go(s, carry):
-            at = jnp.minimum(first_at + s, cap - 1)
-            fwd[j * slots + s] = jnp.where(s < tops[j], held[at], jnp.zeros(held.shape[1:], BF16))
-            return carry
-
-        lax.fori_loop(0, slots, go, 0)
-        if j < half - 1:
-            onward[j].start()
-        else:
-            own[1].start()
-
-    def last_chunk(j):
-        return (min(cap, (j + 1) * slots) - 1) // part
+    def unpack(k):
+        size = ends[k] - starts[k]
+        for i in range(PAIR):
+            listed(i, k).wait_recv()
+            held[i, starts[k]:ends[k]] = relay[i, starts[k]:ends[k]]
+            bits = meta[host * chips + holders[i]]
+            here = lax.broadcasted_iota(I32, bits.shape, 1)
+            for step_, j, low, high in passes(half, slots, ends):
+                if step_ != k:
+                    continue
+                first_at = jnp.sum(jnp.where((here >= count) & (here < count + j), bits, 0))
+                number = jnp.sum(jnp.where(here == count + j, bits, 0))
+
+                def go(s, carry):
+                    at = jnp.minimum(first_at + s, cap - 1)
+                    block = held[i, at]
+                    fwd[i, j * slots + s] = jnp.where(s < number, block, jnp.zeros_like(block))
+                    return carry
+
+                lax.fori_loop(low, high, go, 0)
+                onward[i, k, j].start()
 
     at_lane = lax.broadcasted_iota(I32, (1, 128), 1)
     for d in range(depth):
@@ -309,14 +349,10 @@
         order[d:d + 1, :] = values.astype(F32)
     where = order[...].T[0:SLAB].astype(I32)
 
-    def unpack(k):
-        lists[k].wait_recv()
-        held[k * part:(k + 1) * part] = relay[k * part:(k + 1) * part]
-        for j in range(half):
-            if last_chunk(j) == k:
-                forward(j)
-
-    unpack(0)
+    @pl.when(gate)
+    def _():
+        unpack(0)
+        unpack(1)
 
     pieces[total:, :] = jnp.zeros((pieces.shape[0] - total, pieces.shape[1]), F32)
     rows_wait("recv")
@@ -350,6 +386,10 @@
         return carry
 
     lax.fori_loop(0, batch // 16, products, 0, unroll=2)
+
+    @pl.when(gate)
+    def _():
+        unpack(2)
 
     lane_j = lax.broadcasted_iota(I32, (edge, edge), 0) // 8
     out_lane = lax.broadcasted_iota(I32, (edge, edge), 1)
@@ -385,8 +425,9 @@
     losses[me] = loss_send[0]
     loss_go()
 
-    for k in range(1, CHUNKS):
-        unpack(k)
+    @pl.when(gate)
+    def _():
+        unpack(3)
 
     crossing = jnp.where(at_lane == count + half, jnp.max(meta[...].astype(F32), axis=0), 0.0)
     over_ref[0] = (jnp.max(crossing) > cap).astype(I32)
@@ -398,10 +439,25 @@
     loss_wait("send")
     for c in lists:
         c.wait_send()
-    for c in near + onward:
+    for c in near:
         c.wait()
-    for c in own:
-        c.wait()
+    own.wait()
+
+    @pl.when(gate)
+    def _():
+        for k, j, low, high in passes(half, slots, ends):
+            for i in range(PAIR):
+                onward[i, k, j].wait_send() if j < half - 1 else onward[i, k, j].wait()
+
+    for k, j, low, high in passes(half, slots, ends):
+        if j == half - 1:
+            continue
+        source = lax.rem(local - turn(j, half)[0] + half_chips, half_chips)
+
+        @pl.when(lax.rem(source, PAIR) == 1 - my_half)
+        def _():
+            for i in range(PAIR):
+                onward[i, k, j].wait_recv()
 
 
 def step(hosts, chips, slots, bl, arrays):
@@ -413,15 +469,15 @@
     count = homes + orphs
     batch = arrays["dense"].shape[1]
     top = arrays["wt"].shape[1]
-    cap = -(-3 * orphs // (4 * CHUNKS)) * CHUNKS
+    cap = -(-11 * orphs // 16)
     total = devices * count
     depth = -(-total // (F * 128)) * 128
     dma = pltpu.SemaphoreType.DMA
     scratch = [VM(arrays[n].shape, arrays[n].dtype) for n in NAMES] + [
         VM((half * slots + cap, height, width), BF16),
-        VM((cap, height, width), BF16),
-        VM((cap, height, width), BF16),
-        VM((half * slots, height, width), BF16),
+        VM((PAIR, cap, height, width), BF16),
+        VM((PAIR, cap, height, width), BF16),
+        VM((PAIR, half * slots, height, width), BF16),
         VM((devices, 1, 128), I32),
         VM((devices, 1, 128), I32),
         VM((128, 128), F32),
@@ -439,9 +495,9 @@
         VM((devices, 1, 128), F32),
         dma((len(NAMES),)),
         dma((devices,)), dma((devices,)), dma((devices,)), dma((devices,)), dma((devices,)), dma((devices,)),
-        dma((CHUNKS,)), dma((CHUNKS,)),
-        dma((half,)), dma((half,)), dma((half,)), dma((half,)),
-        dma((2,)),
+        dma((4,)), dma((PAIR, 4)),
+        dma((half,)), dma((half,)), dma((PAIR, 2 * half + 4)), dma((PAIR, 2 * half + 4)),
+        dma,
     ]
     smem, hbm, vmem = (pl.BlockSpec(memory_space=m) for m in (SMEM, HBM, VM))
     return pl.pallas_call(

time: 68.1 us -> 72.7 us (1.068); the launches traced: 67.9 us -> 71.8 us
  Pallas kernels: 62.4 us -> 66.2 us
    pallas_call x1, Pallas kernels: 62.4 us -> 66.2 us  [step(): pl.pallas_call(functools.partial(step_kernel, hosts, chips, slots, cap, d...]
where the time goes in v1:
time: 72.7 us; the launch traced here: 71.8 us
  Pallas kernels  66.2 us (91%)
  between operations  3.67 us (5%)
  local copies, waits for them, and re-layouts  1.91 us (3%)
    pallas_call x1, Pallas kernels, step(): pl.pallas_call(functools.partial(step_kernel, hosts, chips, slots, cap, d...  66.2 us
    unnamed x8, local copies, waits for them, and re-layouts  1.91 us

profile of v1, /device:TPU:1, one launch (start us, length us, event | category | flops | bytes accessed | tf_op | source)
XLA Modules:
  0.0 71.8 jit_solution(17452486898753743773)
XLA Ops:
  1.3 0.0 copy-start
  1.3 0.0 copy-start.2
  1.3 66.2 %step.1 = (bf16[64,128,128]{2,1,0:T(8,128)(2,1)S(1)}, f32[1,512]{1,0:T(1,128)}, f32[1]{0:T(128)}, s32[1]{0:T(128)}) custom-call(f32[1]{0:T(128)S(6)} %copy.29.refs_0_, s32[1,32]{1,0:T(1,128)} %bitcast.34, bf16[32,128,128]{2,1,0:T(8,128)(2,1)} %refs_2_.1, bf16[48,128,128]{2,1,0:T(8,128)(2,1)} %refs_3_.1, s32[32,8,48]{2,1,0:T(8,128)} %bitcast.23, ...), custom_call_target="tpu_custom_call" | custom-call | flops 8000000000 | bytes 8000000 | tf_op jit(solution)/shard_map/step/pallas_call | solution.py:503
  68.2 0.0 copy-done
  68.2 0.0 copy-done.2
  68.2 0.0 copy-start.1
  68.2 1.3 %copy.30 = bf16[64,128,128]{2,1,0:T(8,128)(2,1)} copy(bf16[64,128,128]{2,1,0:T(8,128)(2,1)S(1)} %get-tuple-element.31) | data formatting | bytes 4194304
  69.5 0.0 copy-done.1
  69.5 0.6 copy.31
  (1 shorter events, 0.0 us)
Async XLA Ops:
  1.3 66.9 %copy-start = (bf16[32,128,128]{2,1,0:T(8,128)(2,1)S(1)}, bf16[32,128,128]{2,1,0:T(8,128)(2,1)}, u32[]{:S(2)}) copy-start(bf16[32,128,128]{2,1,0:T(8,128)(2,1)} %refs_2_.1) | copy-start | bytes 3145732
  1.3 66.9 %copy-start.2 = (s32[32,1]{0,1:T(1,128)S(1)}, s32[32,1]{0,1:T(1,128)}, u32[]{:S(2)}) copy-start(s32[32,1]{0,1:T(1,128)} %param.31) | copy-start | bytes 388
  68.2 1.3 %copy-start.1 = (f32[1,512]{1,0:T(1,128)S(1)}, f32[1,512]{1,0:T(1,128)}, u32[]{:S(2)}) copy-start(f32[1,512]{1,0:T(1,128)} %get-tuple-element.22) | copy-start | bytes 6148

commit v2 on v1

--- a/solution.py
+++ b/solution.py
@@ -69,8 +69,7 @@
     v = dict(zip(NAMES, refs[4:4 + len(NAMES)]))
     (packed, relay, held, fwd, meta_send, meta, stage, counts, rows, out_rows, arrived, pieces, slab, gram, wpad, wexp,
      order, loss_send, losses,
-     in_sems, meta_s, meta_r, row_s, row_r, loss_s, loss_r, list_s, list_r, near_s, near_r, fwd_s, fwd_r,
-     own_sem) = refs[4 + len(NAMES):]
+     in_sems, meta_s, meta_r, row_s, row_r, loss_s, loss_r, list_s, list_r, near_s, near_r, fwd_s, fwd_r) = refs[4 + len(NAMES):]
 
     homes, height = v["home"].shape[0], v["home"].shape[1]
     orphs = v["orph"].shape[0]
@@ -95,43 +94,38 @@
     holders = [across + (low_chip + i) * CORES + core for i in range(PAIR)]
     turn_in = lax.rem(local, PAIR)
 
-    def peer(e):
-        side, e = lax.div(e, hosts * half), lax.rem(e, hosts * half)
-        dh, e = lax.div(e, half), lax.rem(e, half)
-        return lax.rem(host + dh, hosts), walk(chip, half, side, lax.div(e, CORES), lax.rem(e, CORES))
-
+    at_host = [lax.rem(host + dh, hosts) for dh in range(hosts)]
+    at_chip = [walk(chip, half, side, k // CORES, k % CORES) for side in range(2) for k in range(half)]
+    peers = [(at_host[dh], at_chip[side * half + k])
+             for side in range(2) for dh in range(hosts) for k in range(half)]
+    others = [(e, *peers[e]) for e in range(devices - 1, 0, -1)]
+
+    loads = {n: pltpu.make_async_copy(hbm[n], v[n], in_sems.at[k]) for k, n in enumerate(NAMES)}
+    for n in NAMES[:2]:
+        loads[n].start()
     bar = pltpu.get_barrier_semaphore()
 
-    def hello(e, carry):
-        pl.semaphore_signal(bar, 1, device_id=peer(e), device_id_type=MESH)
-        return carry
-
-    lax.fori_loop(1, devices, hello, 0)
-
-    loads = {n: pltpu.make_async_copy(hbm[n], v[n], in_sems.at[k]) for k, n in enumerate(NAMES)}
-    for n in NAMES:
+    for _, h, c in others:
+        pl.semaphore_signal(bar, 1, device_id=(h, c), device_id_type=MESH)
+    for n in NAMES[2:]:
         loads[n].start()
 
     def everyone(src, dst, send, recv, indexed):
-        def copy(e):
-            h, c = peer(e)
-            return pltpu.make_async_remote_copy(
+        copies = [
+            pltpu.make_async_remote_copy(
                 src_ref=src.at[h * chips + c] if indexed else src.at[0],
                 dst_ref=dst.at[me], send_sem=send.at[e], recv_sem=recv.at[e],
                 device_id=(h, c), device_id_type=MESH)
+            for e, h, c in others
+        ]
 
         def start():
-            def go(i, carry):
-                copy(devices - i).start()
-                return carry
-            lax.fori_loop(1, devices, go, 0)
+            for copy in copies:
+                copy.start()
 
         def wait(kind):
-            def go(i, carry):
-                c = copy(devices - i)
-                c.wait_recv() if kind == "recv" else c.wait_send()
-                return carry
-            lax.fori_loop(1, devices, go, 0)
+            for copy in copies:
+                copy.wait_recv() if kind == "recv" else copy.wait_send()
 
         return start, wait
 
@@ -169,12 +163,6 @@
         for i in range(PAIR):
             if j < half - 1:
                 onward[i, k, j] = group(fwd.at[i], holders[i], j, low, high, fwd_s.at[i, n], fwd_r.at[i, n])
-            else:
-                onward[i, k, j] = pltpu.make_async_copy(
-                    fwd.at[i, pl.ds(j * slots + low, high - low)],
-                    rehomed.at[pl.ds(holders[i] * slots + low, high - low)], fwd_s.at[i, n])
-    own = pltpu.make_async_copy(packed.at[pl.ds((half - 1) * slots, slots)],
-                                rehomed.at[pl.ds(chip * slots, slots)], own_sem)
 
     loads["owner"].wait()
     to = v["owner"][...]
@@ -191,8 +179,6 @@
     prefix = jnp.sum((kind.T < kind).astype(F32), axis=0, keepdims=True).astype(I32)
     inside = jnp.sum((kind.T < half).astype(F32), axis=0, keepdims=True).astype(I32)
     place = jnp.where(key < half, key * slots + rank - prefix, half * slots + rank - inside)
-    sizes = [jnp.sum((key == half + j).astype(I32)) for j in range(half)]
-    sizes.append(jnp.sum((key >= half).astype(I32)))
     loads["orph"].wait()
 
     def pack(first_at, number):
@@ -204,15 +190,8 @@
     pack(half * slots, ends[0])
     pl.semaphore_wait(bar, devices - 1)
     lists[0].start()
-    pack(half * slots + starts[1], ends[1] - starts[1])
-    lists[1].start()
-    pack(0, half * slots)
-    near[0].start()
-    for j in range(half - CORES, half - 1):
-        near[j].start()
-    own.start()
-    pack(half * slots + starts[2], cap - starts[2])
-
+    sizes = [jnp.sum((key == half + j).astype(I32)) for j in range(half)]
+    sizes.append(jnp.sum((key >= half).astype(I32)))
     stage[...] = jnp.zeros_like(stage)
     loads["osamp"].wait()
     stage[0:orphs, 0:devices] = v["osamp"][...].astype(F32)
@@ -230,6 +209,13 @@
 
     meta_go()
 
+    pack(0, half * slots)
+    near[0].start()
+    for j in range(half - CORES, half - 1):
+        near[j].start()
+    rehomed[pl.ds(chip * slots, slots)] = packed[(half - 1) * slots:half * slots]
+    pack(half * slots + starts[1], cap - starts[1])
+
     row = lax.broadcasted_iota(I32, (height, 128), 0)
     bag = hbm["hoff"].shape[1]
 
@@ -282,11 +268,8 @@
     lax.fori_loop(0, orphs // per, orph_group, 0)
     out_rows[...] = rows[...].reshape(out_rows.shape).astype(BF16)
     rows_go()
+
     arrived[me] = out_rows[me]
-    for k in range(2, steps):
-        lists[k].start()
-    for j in range(1, half - CORES):
-        near[j].start()
 
     for n in NAMES[9:]:
         loads[n].wait()
@@ -323,11 +306,16 @@
                 def go(s, carry):
                     at = jnp.minimum(first_at + s, cap - 1)
                     block = held[i, at]
-                    fwd[i, j * slots + s] = jnp.where(s < number, block, jnp.zeros_like(block))
+                    block = jnp.where(s < number, block, jnp.zeros_like(block))
+                    if j < half - 1:
+                        fwd[i, j * slots + s] = block
+                    else:
+                        rehomed[holders[i] * slots + s] = block
                     return carry
 
                 lax.fori_loop(low, high, go, 0)
-                onward[i, k, j].start()
+                if j < half - 1:
+                    onward[i, k, j].start()
 
     at_lane = lax.broadcasted_iota(I32, (1, 128), 1)
     for d in range(depth):
@@ -352,10 +340,14 @@
     @pl.when(gate)
     def _():
         unpack(0)
-        unpack(1)
 
     pieces[total:, :] = jnp.zeros((pieces.shape[0] - total, pieces.shape[1]), F32)
     rows_wait("recv")
+
+    lists[1].start()
+    lists[2].start()
+    for j in range(1, half - CORES):
+        near[j].start()
 
     def settle(p, carry):
         pieces[pl.ds(pl.multiple_of(p * homes, 8), homes), :] = arrived[p, 0:homes].astype(F32)
@@ -389,7 +381,7 @@
 
     @pl.when(gate)
     def _():
-        unpack(2)
+        unpack(1)
 
     lane_j = lax.broadcasted_iota(I32, (edge, edge), 0) // 8
     out_lane = lax.broadcasted_iota(I32, (edge, edge), 1)
@@ -424,9 +416,11 @@
     loss_send[0] = jnp.broadcast_to(loss, (1, 128))
     losses[me] = loss_send[0]
     loss_go()
+    lists[3].start()
 
     @pl.when(gate)
     def _():
+        unpack(2)
         unpack(3)
 
     crossing = jnp.where(at_lane == count + half, jnp.max(meta[...].astype(F32), axis=0), 0.0)
@@ -441,13 +435,12 @@
         c.wait_send()
     for c in near:
         c.wait()
-    own.wait()
 
     @pl.when(gate)
     def _():
         for k, j, low, high in passes(half, slots, ends):
-            for i in range(PAIR):
-                onward[i, k, j].wait_send() if j < half - 1 else onward[i, k, j].wait()
+            for i in range(PAIR if j < half - 1 else 0):
+                onward[i, k, j].wait_send()
 
     for k, j, low, high in passes(half, slots, ends):
         if j == half - 1:
@@ -469,7 +462,7 @@
     count = homes + orphs
     batch = arrays["dense"].shape[1]
     top = arrays["wt"].shape[1]
-    cap = -(-11 * orphs // 16)
+    cap = -(-3 * orphs // 4)
     total = devices * count
     depth = -(-total // (F * 128)) * 128
     dma = pltpu.SemaphoreType.DMA
@@ -497,7 +490,6 @@
         dma((devices,)), dma((devices,)), dma((devices,)), dma((devices,)), dma((devices,)), dma((devices,)),
         dma((4,)), dma((PAIR, 4)),
         dma((half,)), dma((half,)), dma((PAIR, 2 * half + 4)), dma((PAIR, 2 * half + 4)),
-        dma,
     ]
     smem, hbm, vmem = (pl.BlockSpec(memory_space=m) for m in (SMEM, HBM, VM))
     return pl.pallas_call(
@@ -509,13 +501,41 @@
             jax.ShapeDtypeStruct((1,), I32),
         ),
         in_specs=[smem] + [hbm] * len(NAMES),
-        out_specs=(hbm, vmem, smem, smem),
+        out_specs=(vmem, vmem, smem, smem),
         scratch_shapes=scratch,
         cost_estimate=cost(8_000_000_000, 8_000_000),
         compiler_params=pltpu.CompilerParams(
             collective_id=0, has_side_effects=True, vmem_limit_bytes=56 * 2**20),
         name="step",
     )(bl, *[arrays[n] for n in NAMES])
+
+
+def finish_kernel(parts, rehomed, logits, rehomed_out, logits_out, sems):
+    size = rehomed.shape[0] // parts
+    copies = [
+        pltpu.make_async_copy(rehomed.at[pl.ds(k * size, size)], rehomed_out.at[pl.ds(k * size, size)], sems.at[k])
+        for k in range(parts)
+    ]
+    copies.append(pltpu.make_async_copy(logits, logits_out, sems.at[parts]))
+    for copy in copies:
+        copy.start()
+    for copy in copies:
+        copy.wait()
+
+
+def finish(rehomed, logits, parts=4):
+    vmem, hbm = pl.BlockSpec(memory_space=VM), pl.BlockSpec(memory_space=HBM)
+    return pl.pallas_call(
+        functools.partial(finish_kernel, parts),
+        out_shape=(jax.ShapeDtypeStruct(rehomed.shape, rehomed.dtype),
+                   jax.ShapeDtypeStruct(logits.shape, logits.dtype)),
+        in_specs=[vmem, hbm],
+        out_specs=(hbm, hbm),
+        scratch_shapes=[pltpu.SemaphoreType.DMA((parts + 1,))],
+        cost_estimate=cost(1000, 2 * rehomed.size * 2),
+        compiler_params=pltpu.CompilerParams(vmem_limit_bytes=2 * 2**20),
+        name="finish",
+    )(rehomed, logits)
 
 
 def padded(owners, blocks, chips, slots):
@@ -572,6 +592,7 @@
         lambda r, o, b: r,
         rehomed, owners, orphan_blocks,
     )
+    rehomed, logits = finish(rehomed, logits)
     return rehomed, logits[0], loss[0]
 
 

time: 72.7 us -> 68.6 us (0.944)
  Pallas kernels: 66.2 us -> 63.9 us
  local copies, waits for them, and re-layouts: 1.91 us -> 0.67 us
    pallas_call x1, Pallas kernels: 66.2 us -> 62.5 us  [step(): pl.pallas_call(functools.partial(step_kernel, hosts, chips, slots, cap, d...]
    pallas_call x0 -> x1, Pallas kernels: none -> 1.35 us  [finish(): pl.pallas_call(functools.partial(finish_kernel, parts), out_shape=(jax.Sh...]
    unnamed x8 -> x6, local copies, waits for them, and re-layouts: 1.91 us -> 0.67 us
where the time goes in v2:
time: 68.6 us; the launch traced here: 68.2 us
  Pallas kernels  63.9 us (93%)
  between operations  3.67 us (5%)
    pallas_call x1, Pallas kernels, step(): pl.pallas_call(functools.partial(step_kernel, hosts, chips, slots, cap, d...  62.5 us

profile of v2, /device:TPU:1, one launch (start us, length us, event | category | flops | bytes accessed | tf_op | source)
XLA Modules:
  0.0 68.2 jit_solution(11252264142078304122)
XLA Ops:
  1.3 0.0 copy-start.1
  1.3 0.0 copy-start.2
  1.3 62.5 %step.1 = (bf16[64,128,128]{2,1,0:T(8,128)(2,1)S(1)}, f32[1,512]{1,0:T(1,128)}, f32[1]{0:T(128)}, s32[1]{0:T(128)}) custom-call(f32[1]{0:T(128)S(6)} %copy.27.refs_0_, s32[1,32]{1,0:T(1,128)} %bitcast.34, bf16[32,128,128]{2,1,0:T(8,128)(2,1)} %refs_2_.1, bf16[48,128,128]{2,1,0:T(8,128)(2,1)} %refs_3_.1, s32[32,8,48]{2,1,0:T(8,128)} %bitcast.22, ...), custom_call_target="tpu_custom_call" | custom-call | flops 8000000000 | bytes 8000000 | tf_op jit(solution)/shard_map/step/pallas_call | solution.py:495
  64.5 0.0 copy-done.1
  64.5 0.0 copy-done.2
  64.5 0.0 copy-start
  64.5 0.7 copy-done
  65.2 1.4 %finish.1 = (bf16[64,128,128]{2,1,0:T(8,128)(2,1)}, f32[1,512]{1,0:T(1,128)}) custom-call(bf16[64,128,128]{2,1,0:T(8,128)(2,1)S(1)} %get-tuple-element.35.rehomed, f32[1,512]{1,0:T(1,128)S(1)} %copy-done), custom_call_target="tpu_custom_call" | custom-call | flops 1000 | bytes 4194304 | tf_op jit(solution)/shard_map/finish/pallas_call | solution.py:528
  (1 shorter events, 0.0 us)
Async XLA Ops:
  1.3 63.2 %copy-start.1 = (bf16[32,128,128]{2,1,0:T(8,128)(2,1)S(1)}, bf16[32,128,128]{2,1,0:T(8,128)(2,1)}, u32[]{:S(2)}) copy-start(bf16[32,128,128]{2,1,0:T(8,128)(2,1)} %refs_2_.1) | copy-start | bytes 3145732
  1.3 63.2 %copy-start.2 = (s32[32,1]{0,1:T(1,128)S(1)}, s32[32,1]{0,1:T(1,128)}, u32[]{:S(2)}) copy-start(s32[32,1]{0,1:T(1,128)} %param.31) | copy-start | bytes 388
  64.5 0.7 %copy-start = (f32[1,512]{1,0:T(1,128)S(1)}, f32[1,512]{1,0:T(1,128)}, u32[]{:S(2)}) copy-start(f32[1,512]{1,0:T(1,128)} %get-tuple-element.24.logits) | copy-start | bytes 6148

commit v3 on v2

--- a/solution.py
+++ b/solution.py
@@ -78,7 +78,7 @@
     width = v["home"].shape[2]
     batch = logit_ref.shape[1]
     quarter = orphs // 8
-    ends = [2 * quarter, 3 * quarter, 4 * quarter, cap]
+    ends = [2 * quarter, 3 * quarter, 4 * quarter, 5 * quarter, cap]
     starts = [0] + ends[:-1]
     steps = len(ends)
 
@@ -211,6 +211,12 @@
 
     pack(0, half * slots)
     near[0].start()
+
+    @pl.when(gate)
+    def _():
+        for j in range(1, half - CORES):
+            near[j].start()
+
     for j in range(half - CORES, half - 1):
         near[j].start()
     rehomed[pl.ds(chip * slots, slots)] = packed[(half - 1) * slots:half * slots]
@@ -346,8 +352,12 @@
 
     lists[1].start()
     lists[2].start()
-    for j in range(1, half - CORES):
-        near[j].start()
+    lists[3].start()
+
+    @pl.when(jnp.logical_not(gate))
+    def _():
+        for j in range(1, half - CORES):
+            near[j].start()
 
     def settle(p, carry):
         pieces[pl.ds(pl.multiple_of(p * homes, 8), homes), :] = arrived[p, 0:homes].astype(F32)
@@ -416,12 +426,13 @@
     loss_send[0] = jnp.broadcast_to(loss, (1, 128))
     losses[me] = loss_send[0]
     loss_go()
-    lists[3].start()
+    lists[4].start()
 
     @pl.when(gate)
     def _():
         unpack(2)
         unpack(3)
+        unpack(4)
 
     crossing = jnp.where(at_lane == count + half, jnp.max(meta[...].astype(F32), axis=0), 0.0)
     over_ref[0] = (jnp.max(crossing) > cap).astype(I32)
@@ -462,7 +473,7 @@
     count = homes + orphs
     batch = arrays["dense"].shape[1]
     top = arrays["wt"].shape[1]
-    cap = -(-3 * orphs // 4)
+    cap = -(-24 * orphs // 32)
     total = devices * count
     depth = -(-total // (F * 128)) * 128
     dma = pltpu.SemaphoreType.DMA
@@ -488,8 +499,8 @@
         VM((devices, 1, 128), F32),
         dma((len(NAMES),)),
         dma((devices,)), dma((devices,)), dma((devices,)), dma((devices,)), dma((devices,)), dma((devices,)),
-        dma((4,)), dma((PAIR, 4)),
-        dma((half,)), dma((half,)), dma((PAIR, 2 * half + 4)), dma((PAIR, 2 * half + 4)),
+        dma((5,)), dma((PAIR, 5)),
+        dma((half,)), dma((half,)), dma((PAIR, 2 * half + 5)), dma((PAIR, 2 * half + 5)),
     ]
     smem, hbm, vmem = (pl.BlockSpec(memory_space=m) for m in (SMEM, HBM, VM))
     return pl.pallas_call(
@@ -529,7 +540,7 @@
         functools.partial(finish_kernel, parts),
         out_shape=(jax.ShapeDtypeStruct(rehomed.shape, rehomed.dtype),
                    jax.ShapeDtypeStruct(logits.shape, logits.dtype)),
-        in_specs=[vmem, hbm],
+        in_specs=[vmem, pl.BlockSpec(memory_space=pl.ANY)],
         out_specs=(hbm, hbm),
         scratch_shapes=[pltpu.SemaphoreType.DMA((parts + 1,))],
         cost_estimate=cost(1000, 2 * rehomed.size * 2),

time: 68.6 us -> 67.4 us (0.983)
  Pallas kernels: 63.9 us -> 62.9 us
    pallas_call x1, Pallas kernels: 62.5 us -> 61.5 us  [step(): pl.pallas_call(functools.partial(step_kernel, hosts, chips, slots, cap, d...]
where the time goes in v3:
time: 67.4 us; the launch traced here: 67.2 us
  Pallas kernels  62.9 us (93%)
  between operations  3.67 us (5%)
    pallas_call x1, Pallas kernels, step(): pl.pallas_call(functools.partial(step_kernel, hosts, chips, slots, cap, d...  61.5 us
    pallas_call x1, Pallas kernels, finish(): pl.pallas_call(functools.partial(finish_kernel, parts), out_shape=(jax.Sh...  1.35 us

profile of v3, /device:TPU:1, one launch (start us, length us, event | category | flops | bytes accessed | tf_op | source)
XLA Modules:
  0.0 67.2 jit_solution(12663266881082011938)
XLA Ops:
  1.3 0.0 copy-start.1
  1.3 0.0 copy-start.2
  1.3 61.5 %step.1 = (bf16[64,128,128]{2,1,0:T(8,128)(2,1)S(1)}, f32[1,512]{1,0:T(1,128)}, f32[1]{0:T(128)}, s32[1]{0:T(128)}) custom-call(f32[1]{0:T(128)S(6)} %copy.27.refs_0_, s32[1,32]{1,0:T(1,128)} %bitcast.34, bf16[32,128,128]{2,1,0:T(8,128)(2,1)} %refs_2_.1, bf16[48,128,128]{2,1,0:T(8,128)(2,1)} %refs_3_.1, s32[32,8,48]{2,1,0:T(8,128)} %bitcast.22, ...), custom_call_target="tpu_custom_call" | custom-call | flops 8000000000 | bytes 8000000 | tf_op jit(solution)/shard_map/step/pallas_call | solution.py:506
  63.5 0.0 copy-done.1
  63.5 0.0 copy-done.2
  63.5 0.0 copy-start
  63.5 0.7 copy-done
  64.2 1.4 %finish.1 = (bf16[64,128,128]{2,1,0:T(8,128)(2,1)}, f32[1,512]{1,0:T(1,128)}) custom-call(bf16[64,128,128]{2,1,0:T(8,128)(2,1)S(1)} %get-tuple-element.35.rehomed, f32[1,512]{1,0:T(1,128)S(1)} %copy-done), custom_call_target="tpu_custom_call" | custom-call | flops 1000 | bytes 4194304 | tf_op jit(solution)/shard_map/finish/pallas_call | solution.py:539
  (1 shorter events, 0.0 us)
Async XLA Ops:
  1.3 62.2 %copy-start.1 = (bf16[32,128,128]{2,1,0:T(8,128)(2,1)S(1)}, bf16[32,128,128]{2,1,0:T(8,128)(2,1)}, u32[]{:S(2)}) copy-start(bf16[32,128,128]{2,1,0:T(8,128)(2,1)} %refs_2_.1) | copy-start | bytes 3145732
  1.3 62.2 %copy-start.2 = (s32[32,1]{0,1:T(1,128)S(1)}, s32[32,1]{0,1:T(1,128)}, u32[]{:S(2)}) copy-start(s32[32,1]{0,1:T(1,128)} %param.31) | copy-start | bytes 388
  63.5 0.7 %copy-start = (f32[1,512]{1,0:T(1,128)S(1)}, f32[1,512]{1,0:T(1,128)}, u32[]{:S(2)}) copy-start(f32[1,512]{1,0:T(1,128)} %get-tuple-element.24.logits) | copy-start | bytes 6148
